TPU v7x, 32 devices: a whole 2x2x4 slice. The times are simulated.
32 devices in a mesh: row: 8 (over z, core), col: 4 (over y, x).
Axes of the slice: x: 2, y: 2, z: 4, core: 2. Of those that a mesh axis runs over, the one named last changes fastest.
Arguments:
- energy: float32 [4, 2048, 2048], P('col', 'row'), may hold values from 0.5 to 8
- damage_old: float32 [4, 2048, 2048], P('col', 'row'), may hold values from 0 to 0.8
- crack_seeds: int32 [4, 2048, 2048], P('col', 'row'), may hold values 0 or 1
- irreversible: int32 [4, 2048, 2048], P('col', 'row'), may hold values 0 or 1
- line_inverses: float32 [8, 256, 256], replicated, may hold values from -0.6 to 2.8
- z_inverse: float32 [4, 4], replicated, may hold values from -0.8 to 1.9
Outputs:
- damage: float32 [4, 2048, 2048], P('col', 'row')
- update_norms: float32 [2], replicated
All inputs are finite; a program needn't handle non-finite values. No bound on the sum of `crack_seeds` or of `irreversible` on one device may be relied on, other than what follows from the above.
Results may differ from a plain program's by a relative error of at most 0.0001.
Values sent between devices are 32-bit elements; how exact they have to be, the bound alone decides.
A program may use at most 128 MiB of HBM per device.

v0:
```python
import jax
import jax.numpy as jnp
from jax import lax
from jax.sharding import PartitionSpec as P

ITERS = 2
KAPPA = 2.0
STEP = 0.02
COUPLE = 0.5
EPSILON = 1e-06


def second_difference(grid_field, along):
    extent = grid_field.shape[along]
    forward_diff = lax.slice_in_dim(grid_field, 1, extent, axis=along) - lax.slice_in_dim(
        grid_field, 0, extent - 1, axis=along
    )
    zero_shape = list(grid_field.shape)
    zero_shape[along] = 1
    zero_rim = jnp.zeros(zero_shape, grid_field.dtype)
    ahead = jnp.concatenate([forward_diff, zero_rim], axis=along)
    behind = jnp.concatenate([zero_rim, forward_diff], axis=along)
    return ahead - behind


def line_solve(line_rows, inverses):
    block_count, block_cells, _ = inverses.shape
    line_count = line_rows.shape[0]
    blocks = line_rows.reshape(line_count, block_count, block_cells)
    products = jnp.einsum("rkb,kcb->rkc", blocks, inverses, precision=lax.Precision.HIGHEST)
    first_col = inverses[:, :, 0]
    last_col = inverses[:, :, block_cells - 1]
    incoming = [jnp.zeros((line_count,), line_rows.dtype)]
    for block_index in range(block_count - 1):
        incoming.append(
            products[:, block_index, block_cells - 1]
            + COUPLE * incoming[block_index] * inverses[block_index, block_cells - 1, 0]
        )
    inflow = jnp.stack(incoming, axis=1)
    forward = products + COUPLE * inflow[:, :, None] * first_col[None]
    head_terms = [jnp.zeros((line_count,), line_rows.dtype) for block_index in range(block_count)]
    carried = forward[:, block_count - 1, 0]
    for block_index in range(block_count - 2, -1, -1):
        head_terms[block_index] = carried
        carried = (
            forward[:, block_index, 0]
            + COUPLE * carried * inverses[block_index, 0, block_cells - 1]
        )
    outflow = jnp.stack(head_terms, axis=1)
    solved = forward + COUPLE * outflow[:, :, None] * last_col[None]
    return solved.reshape(line_count, block_count * block_cells)


def local(energy, damage_old, crack_seeds, irreversible, line_inverses, z_inverse):
    planes, rows_here, line_length = energy.shape
    row_count = lax.axis_size("row")
    col_count = lax.axis_size("col")
    total_planes = planes * col_count
    cell_count = total_planes * rows_here * row_count * line_length
    seeded = crack_seeds == 1
    damage = jnp.where(seeded, 1.0, damage_old)
    lower_bound = jnp.where(irreversible == 1, damage_old, 0.0)
    own_sums = []
    for sweep_index in range(ITERS):
        local_lap = second_difference(damage, 2)
        partial_value = energy - (1.0 + energy) * damage + KAPPA * local_lap
        moved_part, moved_damage = (
            lax.all_to_all(
                lax.all_to_all(
                    jnp.swapaxes(partial_value, 1, 2),
                    "row",
                    split_axis=1,
                    concat_axis=2,
                    tiled=True,
                ),
                "col",
                split_axis=1,
                concat_axis=0,
                tiled=True,
            ),
            lax.all_to_all(
                lax.all_to_all(
                    jnp.swapaxes(damage, 1, 2), "row", split_axis=1, concat_axis=2, tiled=True
                ),
                "col",
                split_axis=1,
                concat_axis=0,
                tiled=True,
            ),
        )
        lap_rest = second_difference(moved_damage, 2) + second_difference(moved_damage, 0)
        turned = moved_part + KAPPA * lap_rest
        turned_shape = turned.shape
        along_y = line_solve(turned.reshape(-1, turned_shape[2]), line_inverses).reshape(
            turned_shape
        )
        along_z = jnp.einsum("zk,kxy->zxy", z_inverse, along_y, precision=lax.Precision.HIGHEST)
        gathered = lax.all_to_all(
            lax.all_to_all(along_z, "row", split_axis=2, concat_axis=1, tiled=True),
            "col",
            split_axis=0,
            concat_axis=1,
            tiled=True,
        )
        piece_cells = gathered.shape[1] // (row_count * col_count)
        reordered = gathered.reshape(planes, col_count, row_count, piece_cells, rows_here)
        restored = jnp.transpose(reordered, (0, 4, 2, 1, 3)).reshape(planes, rows_here, line_length)
        update = STEP * line_solve(restored.reshape(-1, line_length), line_inverses).reshape(
            restored.shape
        )
        clamped = jnp.minimum(jnp.maximum(damage + update, lower_bound), 1.0)
        renewed = jnp.where(seeded, 1.0, clamped)
        own_sum = jnp.sum((renewed - damage) ** 2)
        own_sums.append(own_sum)
        damage = renewed
    global_sums = lax.psum(jnp.stack(own_sums), ("row", "col"))
    update_norms = jnp.sqrt(global_sums / cell_count + EPSILON) / STEP
    return (damage, update_norms)


def solution(mesh):
    return jax.shard_map(
        local,
        mesh=mesh,
        in_specs=(
            P("col", "row", None),
            P("col", "row", None),
            P("col", "row", None),
            P("col", "row", None),
            P(),
            P(),
        ),
        out_specs=(P("col", "row", None), P()),
        check_vma=False,
    )
```

profile of v0, /device:TPU:10, one launch (start us, length us, event | category | flops | bytes accessed | tf_op | source)
XLA Modules:
  0.0 739.1 jit_solution(10383993715968311955)
XLA Ops:
  5.4 6.2 copy.149
  11.6 6.4 broadcast_select_fusion.1
  32.9 7.5 %add_bitcast_fusion.1 = f32[1,2048,256]{2,0,1:T(1,128)} fusion(f32[1,256,2047]{1,0,2:T(1,128)S(1)} %slice_subtract_fusion.3, f32[1,256,2048]{1,0,2:T(1,128)S(1)} %copy.151, f32[1,256,2048]{1,0,2:T(1,128)} %broadcast_select_fusion.1), kind=kLoop, calls=%fused_computation.27 | loop fusion | flops 3145728 | bytes 8387584 | tf_op jit(solution)/shard_map/transpose | solution.py:70
  40.4 28.5 %all-to-all-done.2 = f32[1,2048,256]{2,0,1:T(1,128)} async-done(((f32[1,2048,256]{2,0,1:T(1,128)}), f32[1,2048,256]{2,0,1:T(1,128)}, u32[]{:S(2)}, u32[]{:S(2)}) %all-to-all-start.2) | async-done | bytes 2097184 | tf_op jit(solution)/shard_map/all_to_all | solution.py:82
  68.9 7.8 %all-to-all-start = ((f32[1,2048,256]{2,0,1:T(1,128)}), f32[1,2048,256]{2,0,1:T(1,128)}, u32[]{:S(2)}, u32[]{:S(2)}) async-start(f32[1,2048,256]{2,0,1:T(1,128)} %add_bitcast_fusion.1), calls=%async_computation | async-start | bytes 4194304 | tf_op jit(solution)/shard_map/all_to_all | solution.py:69
  80.2 6.1 copy.155
  86.3 35.9 %all-to-all-done = f32[1,2048,256]{2,0,1:T(1,128)} async-done(((f32[1,2048,256]{2,0,1:T(1,128)}), f32[1,2048,256]{2,0,1:T(1,128)}, u32[]{:S(2)}, u32[]{:S(2)}) %all-to-all-start) | async-done | bytes 2097184 | tf_op jit(solution)/shard_map/all_to_all | solution.py:69
  168.6 13.0 %all-to-all-done.1 = f32[1,256,2048]{2,0,1:T(1,128)} async-done(((f32[1,256,2048]{2,0,1:T(1,128)}), f32[1,256,2048]{2,0,1:T(1,128)}, u32[]{:S(2)}, u32[]{:S(2)}) %all-to-all-start.1) | async-done | bytes 2097184 | tf_op jit(solution)/shard_map/all_to_all | solution.py:68
  205.7 6.8 convolution_bitcast_fusion.1
  217.2 7.9 %reshape.1081 = f32[8,1,65536]{2,1,0:T(1,128)} reshape(f32[2048,4,64]{2,1,0:T(4,128)} %bitcast.194) | data formatting | bytes 4194304
  225.1 54.2 %all_to_all.174 = f32[8,1,65536]{2,1,0:T(1,128)} all-to-all(f32[8,1,65536]{2,1,0:T(1,128)} %reshape.1081), channel_id=1, replica_groups=mesh['row'=8,'col'=4] {'row'}, dimensions={0} | all-to-all | bytes 4194304 | tf_op jit(solution)/shard_map/all_to_all | solution.py:99
  279.8 8.6 %reduce = f32[8,65536]{1,0:T(8,128)} reduce(f32[8,1,65536]{2,1,0:T(1,128)} %all_to_all.174, f32[]{:T(128)} %broadcast.872), dimensions={1}, to_apply=%all_to_all.140.reduce_sub_computation | reduce | bytes 4194308 | tf_op jit(solution)/shard_map/all_to_all | solution.py:99
  288.4 6.4 reshape.1082
  311.8 17.4 %all-to-all-done.5 = f32[4,512,256]{2,1,0:T(8,128)} async-done(((f32[4,512,256]{2,1,0:T(8,128)}), f32[4,512,256]{2,1,0:T(8,128)}, u32[]{:S(2)}, u32[]{:S(2)}) %all-to-all-start.5) | async-done | bytes 2097184 | tf_op jit(solution)/shard_map/all_to_all | solution.py:98
  339.6 13.5 %minimum_select_fusion.1 = f32[1,256,2048]{1,0,2:T(1,128)} fusion(f32[1,256,2048]{1,0,2:T(1,128)} %broadcast_select_fusion.1, f32[1,256,2048]{1,2,0:T(8,128)S(1)} %bitcast.215, s32[1,256,2048]{1,0,2:T(1,128)S(1)} %copy-done.3, pred[1,256,2048]{1,0,2:T(4,128)(4,1)} %copy.170, f32[1,256,2048]{1,0,2:T(1,128)S(1)} %copy-done.5), kind=kLoop, calls=%fused_computation.21 | loop fusion | flops 3145728 | bytes 11010048 | tf_op jit(solution)/shard_map/jit(_where)/select_n | solution.py:112
  353.1 6.6 all-to-all-start.8
  364.0 6.6 add_bitcast_fusion
  370.6 34.7 %all-to-all-done.8 = f32[1,2048,256]{2,0,1:T(1,128)} async-done(((f32[1,2048,256]{2,0,1:T(1,128)}), f32[1,2048,256]{2,0,1:T(1,128)}, u32[]{:S(2)}, u32[]{:S(2)}) %all-to-all-start.8) | async-done | bytes 2097184 | tf_op jit(solution)/shard_map/all_to_all | solution.py:82
  405.3 7.8 %all-to-all-start.6 = ((f32[1,2048,256]{2,0,1:T(1,128)}), f32[1,2048,256]{2,0,1:T(1,128)}, u32[]{:S(2)}, u32[]{:S(2)}) async-start(f32[1,2048,256]{2,0,1:T(1,128)} %add_bitcast_fusion), calls=%async_computation.6 | async-start | bytes 4194304 | tf_op jit(solution)/shard_map/all_to_all | solution.py:69
  419.1 6.1 copy.176
  425.2 33.5 %all-to-all-done.6 = f32[1,2048,256]{2,0,1:T(1,128)} async-done(((f32[1,2048,256]{2,0,1:T(1,128)}), f32[1,2048,256]{2,0,1:T(1,128)}, u32[]{:S(2)}, u32[]{:S(2)}) %all-to-all-start.6) | async-done | bytes 2097184 | tf_op jit(solution)/shard_map/all_to_all | solution.py:69
  469.6 6.1 copy.174
  475.7 12.8 %all-to-all-done.9 = f32[1,256,2048]{2,0,1:T(1,128)} async-done(((f32[1,256,2048]{2,0,1:T(1,128)}), f32[1,256,2048]{2,0,1:T(1,128)}, u32[]{:S(2)}, u32[]{:S(2)}) %all-to-all-start.9) | async-done | bytes 2097184 | tf_op jit(solution)/shard_map/all_to_all | solution.py:81
  504.8 13.0 %all-to-all-done.7 = f32[1,256,2048]{2,0,1:T(1,128)} async-done(((f32[1,256,2048]{2,0,1:T(1,128)}), f32[1,256,2048]{2,0,1:T(1,128)}, u32[]{:S(2)}, u32[]{:S(2)}) %all-to-all-start.7) | async-done | bytes 2097184 | tf_op jit(solution)/shard_map/all_to_all | solution.py:68
  541.9 6.8 convolution_bitcast_fusion
  553.4 7.9 %reshape.1083 = f32[8,1,65536]{2,1,0:T(1,128)} reshape(f32[2048,4,64]{2,1,0:T(4,128)} %bitcast.196) | data formatting | bytes 4194304
  561.3 54.3 %all_to_all.175 = f32[8,1,65536]{2,1,0:T(1,128)} all-to-all(f32[8,1,65536]{2,1,0:T(1,128)} %reshape.1083), channel_id=1, replica_groups=mesh['row'=8,'col'=4] {'row'}, dimensions={0} | all-to-all | bytes 4194304 | tf_op jit(solution)/shard_map/all_to_all | solution.py:99
  615.6 8.5 %reduce.1 = f32[8,65536]{1,0:T(8,128)} reduce(f32[8,1,65536]{2,1,0:T(1,128)} %all_to_all.175, f32[]{:T(128)} %broadcast.872), dimensions={1}, to_apply=%all_to_all.157.reduce_sub_computation | reduce | bytes 4194308 | tf_op jit(solution)/shard_map/all_to_all | solution.py:99
  624.1 6.4 reshape.1084
  635.3 28.6 %all_to_all.176 = f32[4,512,256]{2,1,0:T(8,128)S(1)} all-to-all(f32[4,512,256]{2,1,0:T(8,128)} %bitcast.202), channel_id=1, replica_groups=mesh['row'=8,'col'=4] {'col'}, dimensions={0} | all-to-all | bytes 4194304 | tf_op jit(solution)/shard_map/all_to_all | solution.py:98
  672.6 16.7 %multiply_reduce_fusion.1 = (f32[]{:T(128)}, f32[]{:T(128)}, f32[1,256,2048]{1,0,2:T(1,128)}) fusion(f32[1,256,2048]{1,0,2:T(1,128)} %minimum_select_fusion.1, f32[1,256,2048]{1,0,2:T(1,128)} %broadcast_select_fusion.1, pred[1,256,2048]{1,0,2:T(4,128)(4,1)} %copy.170, f32[1,256,2048]{1,0,2:T(1,128)S(1)} %copy-done.6, f32[1,256,2048]{1,2,0:T(8,128)S(1)} %bitcast.218, ...), kind=kLoop, calls=%fused_computation.13 | loop fusion | flops 6291454 | bytes 13107208 | tf_op jit(solution)/shard_map/reduce_sum | solution.py:113
  690.7 41.4 %psum.7 = f32[2]{0:T(128)S(1)} all-reduce(f32[2]{0:T(128)S(1)} %pad_maximum_fusion), channel_id=1, replica_groups=mesh['row'=8,'col'=4] {'row','col'}, use_global_device_ids=true, to_apply=%region_2.3 | all-reduce | flops 2 | bytes 16 | tf_op jit(solution)/shard_map/psum | solution.py:116
  (137 shorter events, 205.6 us)
Async XLA Ops:
  0.6 205.0 %copy-start = (f32[4,4]{1,0:T(4,128)S(1)}, f32[4,4]{1,0:T(4,128)}, u32[]{:S(2)}) copy-start(f32[4,4]{1,0:T(4,128)} %param.11) | copy-start | bytes 196
  5.3 6.2 copy-start.2
  17.9 50.9 %all-to-all-start.2 = ((f32[1,2048,256]{2,0,1:T(1,128)}), f32[1,2048,256]{2,0,1:T(1,128)}, u32[]{:S(2)}, u32[]{:S(2)}) async-start(f32[1,2048,256]{2,0,1:T(1,128)} %bitcast.3), calls=%async_computation.2 | async-start | bytes 4194304 | tf_op jit(solution)/shard_map/all_to_all | solution.py:82
  28.0 4.9 copy-start.11
  68.9 53.4 %all-to-all-start = ((f32[1,2048,256]{2,0,1:T(1,128)}), f32[1,2048,256]{2,0,1:T(1,128)}, u32[]{:S(2)}, u32[]{:S(2)}) async-start(f32[1,2048,256]{2,0,1:T(1,128)} %add_bitcast_fusion.1), calls=%async_computation | async-start | bytes 4194304 | tf_op jit(solution)/shard_map/all_to_all | solution.py:69
  86.3 40.8 %copy-start.1 = (f32[8,256,256]{2,1,0:T(8,128)S(1)}, f32[8,256,256]{2,1,0:T(8,128)}, u32[]{:S(2)}) copy-start(f32[8,256,256]{2,1,0:T(8,128)} %param.10) | copy-start | bytes 6291460
  122.2 29.8 %all-to-all-start.3 = ((f32[1,256,2048]{2,0,1:T(1,128)}), f32[1,256,2048]{2,0,1:T(1,128)}, u32[]{:S(2)}, u32[]{:S(2)}) async-start(f32[1,256,2048]{2,0,1:T(1,128)} %copy.155), calls=%async_computation.3 | async-start | bytes 4194304 | tf_op jit(solution)/shard_map/all_to_all | solution.py:81
  152.0 29.6 %all-to-all-start.1 = ((f32[1,256,2048]{2,0,1:T(1,128)}), f32[1,256,2048]{2,0,1:T(1,128)}, u32[]{:S(2)}, u32[]{:S(2)}) async-start(f32[1,256,2048]{2,0,1:T(1,128)} %copy.153), calls=%async_computation.1 | async-start | bytes 4194304 | tf_op jit(solution)/shard_map/all_to_all | solution.py:68
  181.6 2.6 copy-start.13
  181.6 2.7 copy-start.15
  189.1 1.4 copy-start.8
  299.6 29.6 %all-to-all-start.5 = ((f32[4,512,256]{2,1,0:T(8,128)}), f32[4,512,256]{2,1,0:T(8,128)}, u32[]{:S(2)}, u32[]{:S(2)}) async-start(f32[4,512,256]{2,1,0:T(8,128)} %bitcast.198), calls=%async_computation.5 | async-start | bytes 4194304 | tf_op jit(solution)/shard_map/all_to_all | solution.py:98
  333.3 1.4 copy-start.9
  336.8 2.2 copy-start.3
  336.8 2.8 copy-start.5
  353.1 52.2 %all-to-all-start.8 = ((f32[1,2048,256]{2,0,1:T(1,128)}), f32[1,2048,256]{2,0,1:T(1,128)}, u32[]{:S(2)}, u32[]{:S(2)}) async-start(f32[1,2048,256]{2,0,1:T(1,128)} %bitcast.65), calls=%async_computation.8 | async-start | bytes 4194304 | tf_op jit(solution)/shard_map/all_to_all | solution.py:82
  359.7 4.3 copy-start.12
  405.3 53.4 %all-to-all-start.6 = ((f32[1,2048,256]{2,0,1:T(1,128)}), f32[1,2048,256]{2,0,1:T(1,128)}, u32[]{:S(2)}, u32[]{:S(2)}) async-start(f32[1,2048,256]{2,0,1:T(1,128)} %add_bitcast_fusion), calls=%async_computation.6 | async-start | bytes 4194304 | tf_op jit(solution)/shard_map/all_to_all | solution.py:69
  458.7 29.9 %all-to-all-start.9 = ((f32[1,256,2048]{2,0,1:T(1,128)}), f32[1,256,2048]{2,0,1:T(1,128)}, u32[]{:S(2)}, u32[]{:S(2)}) async-start(f32[1,256,2048]{2,0,1:T(1,128)} %copy.176), calls=%async_computation.9 | async-start | bytes 4194304 | tf_op jit(solution)/shard_map/all_to_all | solution.py:81
  488.6 29.2 %all-to-all-start.7 = ((f32[1,256,2048]{2,0,1:T(1,128)}), f32[1,256,2048]{2,0,1:T(1,128)}, u32[]{:S(2)}, u32[]{:S(2)}) async-start(f32[1,256,2048]{2,0,1:T(1,128)} %copy.174), calls=%async_computation.7 | async-start | bytes 4194304 | tf_op jit(solution)/shard_map/all_to_all | solution.py:68
  517.8 2.6 copy-start.14
  517.8 2.7 copy-start.16
  525.3 1.4 copy-start.10
  666.3 1.4 copy-start.7
  669.8 2.2 copy-start.4
  669.8 2.8 copy-start.6
where the time goes:
time: 748 us; the launch traced here: 739 us
  waiting for transfers between devices  190 us (25%)
  blocking collectives  178 us (24%)
  local copies, waits for them, and re-layouts  174 us (23%)
  other arithmetic  110 us (15%)
  starting transfers between devices  53.5 us (7%)
  matrix products  24 us (3%)
  between operations  9.76 us (1%)
    all_to_all x2, blocking collectives, local(): lax.all_to_all(along_z, 'row', split_axis=2, concat_axis=1, tiled=True)  108 us
    unnamed x54, local copies, waits for them, and re-layouts  81.7 us
    all_to_all x2, waiting for transfers between devices, local(): lax.all_to_all(jnp.swapaxes(partial_value, 1, 2), 'row', split_axis=1, co...  69.4 us
    all_to_all x2, waiting for transfers between devices, local(): lax.all_to_all(jnp.swapaxes(damage, 1, 2), 'row', split_axis=1, concat_ax...  63.1 us
    psum x1, blocking collectives, local(): global_sums = lax.psum(jnp.stack(own_sums), ('row', 'col'))  41.4 us
    all_to_all x1, blocking collectives, local(): lax.all_to_all(lax.all_to_all(along_z, 'row', split_axis=2, concat_axis=1...  28.6 us
    all_to_all x2, waiting for transfers between devices, local(): lax.all_to_all(lax.all_to_all(jnp.swapaxes(partial_value, 1, 2), 'row', s...  26 us
    another operation x4, local copies, waits for them, and re-layouts, local(): line_solve(turned.reshape(-1, turned_shape[2]), line_inverses)  20.3 us
  transfers between devices with their start and end apart: 9, of which 9 were waited for; matrix products, arithmetic and copies ran while one was open for 14% of the time, Pallas kernels for 0%

commit v1 on v0

--- a/solution.py
+++ b/solution.py
@@ -79,8 +79,16 @@
                 tiled=True,
             ),
             lax.all_to_all(
-                lax.all_to_all(
-                    jnp.swapaxes(damage, 1, 2), "row", split_axis=1, concat_axis=2, tiled=True
+                jnp.concatenate(
+                    lax.all_to_all(
+                        jnp.stack(
+                            jnp.split(jnp.swapaxes(damage, 1, 2), lax.axis_size("row"), axis=1)
+                        ),
+                        "row",
+                        0,
+                        0,
+                    ),
+                    axis=2,
                 ),
                 "col",
                 split_axis=1,

time: 748 us -> 775 us (1.036)
  local copies, waits for them, and re-layouts: 174 us -> 193 us
  waiting for transfers between devices: 190 us -> 203 us
  other arithmetic: 110 us -> 102 us
    another operation x0 -> x6, local copies, waits for them, and re-layouts: none -> 22.8 us  [local(): jnp.stack(jnp.split(jnp.swapaxes(damage, 1, 2), lax.axis_size('row'), axi...]
    all_to_all x4 -> x0, local copies, waits for them, and re-layouts: 17 us -> none  [local(): lax.all_to_all(jnp.swapaxes(damage, 1, 2), 'row', split_axis=1, concat_ax...]
    reshape x0 -> x2, local copies, waits for them, and re-layouts: none -> 12.3 us  [local(): jnp.concatenate(lax.all_to_all(jnp.stack(jnp.split(jnp.swapaxes(damage, 1...]
    all_to_all x2, waiting for transfers between devices: 69.4 us -> 78.9 us  [local(): lax.all_to_all(jnp.swapaxes(partial_value, 1, 2), 'row', split_axis=1, co...]
    unnamed x54 -> x62, local copies, waits for them, and re-layouts: 81.7 us -> 80.4 us
  transfers between devices with their start and end apart: 9 -> 9, of which waited for: 9 -> 8; matrix products, arithmetic and copies ran while one was open for 14% -> 13% of each run, Pallas kernels for 0% -> 0%
where the time goes in v1:
time: 775 us; the launch traced here: 764 us
  waiting for transfers between devices  203 us (26%)
  local copies, waits for them, and re-layouts  193 us (25%)
  blocking collectives  178 us (23%)
  other arithmetic  102 us (13%)
  starting transfers between devices  53.1 us (7%)
  matrix products  24 us (3%)
  between operations  9.94 us (1%)
    all_to_all x2, blocking collectives, local(): lax.all_to_all(along_z, 'row', split_axis=2, concat_axis=1, tiled=True)  108 us
    unnamed x62, local copies, waits for them, and re-layouts  80.4 us
    all_to_all x2, waiting for transfers between devices, local(): lax.all_to_all(jnp.swapaxes(partial_value, 1, 2), 'row', split_axis=1, co...  78.9 us
    all_to_all x2, waiting for transfers between devices, local(): lax.all_to_all(jnp.stack(jnp.split(jnp.swapaxes(damage, 1, 2), lax.axis_s...  67.4 us
    psum x1, blocking collectives, local(): global_sums = lax.psum(jnp.stack(own_sums), ('row', 'col'))  41.4 us
    all_to_all x1, blocking collectives, local(): lax.all_to_all(lax.all_to_all(along_z, 'row', split_axis=2, concat_axis=1...  28.6 us
    all_to_all x2, waiting for transfers between devices, local(): lax.all_to_all(lax.all_to_all(jnp.swapaxes(partial_value, 1, 2), 'row', s...  26.8 us
    another operation x6, local copies, waits for them, and re-layouts, local(): jnp.stack(jnp.split(jnp.swapaxes(damage, 1, 2), lax.axis_size('row'), axi...  22.8 us
  transfers between devices with their start and end apart: 9, of which 8 were waited for; matrix products, arithmetic and copies ran while one was open for 13% of the time, Pallas kernels for 0%

profile of v1, /device:TPU:10, one launch (start us, length us, event | category | flops | bytes accessed | tf_op | source)
XLA Modules:
  0.0 763.7 jit_solution(15732183006691959410)
XLA Ops:
  0.7 6.2 copy.204
  17.7 6.2 stack.261
  46.0 31.8 %all-to-all-done.2 = f32[8,1,256,256]{2,3,1,0:T(8,128)} async-done(((f32[8,1,256,256]{2,3,1,0:T(8,128)}), f32[8,1,256,256]{2,3,1,0:T(8,128)}, u32[]{:S(2)}, u32[]{:S(2)}) %all-to-all-start.2) | async-done | bytes 2097184 | tf_op jit(solution)/shard_map/all_to_all | solution.py:83
  77.8 7.8 %all-to-all-start = ((f32[1,2048,256]{2,0,1:T(1,128)}), f32[1,2048,256]{2,0,1:T(1,128)}, u32[]{:S(2)}, u32[]{:S(2)}) async-start(f32[1,2048,256]{2,0,1:T(1,128)} %add_bitcast_fusion.1), calls=%async_computation | async-start | bytes 4194304 | tf_op jit(solution)/shard_map/all_to_all | solution.py:69
  85.6 6.1 copy.212
  91.7 39.5 %all-to-all-done = f32[1,2048,256]{2,0,1:T(1,128)} async-done(((f32[1,2048,256]{2,0,1:T(1,128)}), f32[1,2048,256]{2,0,1:T(1,128)}, u32[]{:S(2)}, u32[]{:S(2)}) %all-to-all-start) | async-done | bytes 2097184 | tf_op jit(solution)/shard_map/all_to_all | solution.py:69
  156.7 6.1 copy.209
  178.9 13.8 %all-to-all-done.1 = f32[1,256,2048]{2,0,1:T(1,128)} async-done(((f32[1,256,2048]{2,0,1:T(1,128)}), f32[1,256,2048]{2,0,1:T(1,128)}, u32[]{:S(2)}, u32[]{:S(2)}) %all-to-all-start.1) | async-done | bytes 2097184 | tf_op jit(solution)/shard_map/all_to_all | solution.py:68
  217.4 6.9 convolution_bitcast_fusion.1
  229.0 7.9 %reshape.1097 = f32[8,1,65536]{2,1,0:T(1,128)} reshape(f32[2048,4,64]{2,1,0:T(4,128)} %bitcast.230) | data formatting | bytes 4194304
  236.9 54.1 %all_to_all.148 = f32[8,1,65536]{2,1,0:T(1,128)} all-to-all(f32[8,1,65536]{2,1,0:T(1,128)} %reshape.1097), channel_id=1, replica_groups=mesh['row'=8,'col'=4] {'row'}, dimensions={0} | all-to-all | bytes 4194304 | tf_op jit(solution)/shard_map/all_to_all | solution.py:107
  291.6 8.6 %reduce = f32[8,65536]{1,0:T(8,128)} reduce(f32[8,1,65536]{2,1,0:T(1,128)} %all_to_all.148, f32[]{:T(128)} %broadcast.872), dimensions={1}, to_apply=%all_to_all.117.reduce_sub_computation | reduce | bytes 4194308 | tf_op jit(solution)/shard_map/all_to_all | solution.py:107
  300.2 6.4 reshape.1098
  323.7 17.3 %all-to-all-done.5 = f32[4,512,256]{2,1,0:T(8,128)} async-done(((f32[4,512,256]{2,1,0:T(8,128)}), f32[4,512,256]{2,1,0:T(8,128)}, u32[]{:S(2)}, u32[]{:S(2)}) %all-to-all-start.5) | async-done | bytes 2097184 | tf_op jit(solution)/shard_map/all_to_all | solution.py:106
  351.8 12.5 %minimum_select_fusion.1 = f32[1,256,2048]{1,0,2:T(1,128)S(1)} fusion(f32[1,256,2048]{1,0,2:T(1,128)S(1)} %broadcast_select_fusion.1, f32[1,256,2048]{1,2,0:T(8,128)S(1)} %bitcast.247, s32[1,256,2048]{1,0,2:T(1,128)S(1)} %copy-done.8, pred[1,256,2048]{1,0,2:T(4,128)(4,1)} %copy.227, f32[1,256,2048]{1,0,2:T(1,128)S(1)} %copy-done.10), kind=kLoop, calls=%fused_computation.21 | loop fusion | flops 3145728 | bytes 11010048 | tf_op jit(solution)/shard_map/jit(_where)/select_n | solution.py:120
  366.6 6.2 stack.303
  375.8 6.6 all-to-all-start.8
  392.3 35.6 %all-to-all-done.8 = f32[8,1,256,256]{2,3,1,0:T(8,128)} async-done(((f32[8,1,256,256]{2,3,1,0:T(8,128)}), f32[8,1,256,256]{2,3,1,0:T(8,128)}, u32[]{:S(2)}, u32[]{:S(2)}) %all-to-all-start.8) | async-done | bytes 2097184 | tf_op jit(solution)/shard_map/all_to_all | solution.py:83
  427.9 7.8 %all-to-all-start.6 = ((f32[1,2048,256]{2,0,1:T(1,128)}), f32[1,2048,256]{2,0,1:T(1,128)}, u32[]{:S(2)}, u32[]{:S(2)}) async-start(f32[1,2048,256]{2,0,1:T(1,128)} %add_bitcast_fusion), calls=%async_computation.6 | async-start | bytes 4194304 | tf_op jit(solution)/shard_map/all_to_all | solution.py:69
  435.8 6.1 copy.234
  441.9 39.4 %all-to-all-done.6 = f32[1,2048,256]{2,0,1:T(1,128)} async-done(((f32[1,2048,256]{2,0,1:T(1,128)}), f32[1,2048,256]{2,0,1:T(1,128)}, u32[]{:S(2)}, u32[]{:S(2)}) %all-to-all-start.6) | async-done | bytes 2097184 | tf_op jit(solution)/shard_map/all_to_all | solution.py:69
  492.3 6.1 copy.231
  498.4 12.8 %all-to-all-done.9 = f32[1,256,2048]{2,0,1:T(1,128)} async-done(((f32[1,256,2048]{2,0,1:T(1,128)}), f32[1,256,2048]{2,0,1:T(1,128)}, u32[]{:S(2)}, u32[]{:S(2)}) %all-to-all-start.9) | async-done | bytes 2097184 | tf_op jit(solution)/shard_map/all_to_all | solution.py:81
  527.4 13.0 %all-to-all-done.7 = f32[1,256,2048]{2,0,1:T(1,128)} async-done(((f32[1,256,2048]{2,0,1:T(1,128)}), f32[1,256,2048]{2,0,1:T(1,128)}, u32[]{:S(2)}, u32[]{:S(2)}) %all-to-all-start.7) | async-done | bytes 2097184 | tf_op jit(solution)/shard_map/all_to_all | solution.py:68
  565.3 6.8 convolution_bitcast_fusion
  576.9 7.9 %reshape.1099 = f32[8,1,65536]{2,1,0:T(1,128)} reshape(f32[2048,4,64]{2,1,0:T(4,128)} %bitcast.232) | data formatting | bytes 4194304
  584.7 54.3 %all_to_all.149 = f32[8,1,65536]{2,1,0:T(1,128)} all-to-all(f32[8,1,65536]{2,1,0:T(1,128)} %reshape.1099), channel_id=1, replica_groups=mesh['row'=8,'col'=4] {'row'}, dimensions={0} | all-to-all | bytes 4194304 | tf_op jit(solution)/shard_map/all_to_all | solution.py:107
  639.0 8.6 %reduce.1 = f32[8,65536]{1,0:T(8,128)} reduce(f32[8,1,65536]{2,1,0:T(1,128)} %all_to_all.149, f32[]{:T(128)} %broadcast.872), dimensions={1}, to_apply=%all_to_all.131.reduce_sub_computation | reduce | bytes 4194308 | tf_op jit(solution)/shard_map/all_to_all | solution.py:107
  647.6 6.4 reshape.1100
  658.8 28.6 %all_to_all.150 = f32[4,512,256]{2,1,0:T(8,128)S(1)} all-to-all(f32[4,512,256]{2,1,0:T(8,128)} %bitcast.238), channel_id=1, replica_groups=mesh['row'=8,'col'=4] {'col'}, dimensions={0} | all-to-all | bytes 4194304 | tf_op jit(solution)/shard_map/all_to_all | solution.py:106
  697.6 16.4 %multiply_reduce_fusion.1 = (f32[]{:T(128)}, f32[]{:T(128)}, f32[1,256,2048]{1,0,2:T(1,128)}) fusion(f32[1,256,2048]{1,0,2:T(1,128)S(1)} %copy-done.3, f32[1,256,2048]{1,0,2:T(1,128)S(1)} %broadcast_select_fusion.1, pred[1,256,2048]{1,0,2:T(4,128)(4,1)} %copy.227, f32[1,256,2048]{1,0,2:T(1,128)} %copy.205, f32[1,256,2048]{1,2,0:T(8,128)S(1)} %bitcast.250, ...), kind=kLoop, calls=%fused_computation.13 | loop fusion | flops 6291454 | bytes 13107208 | tf_op jit(solution)/shard_map/reduce_sum | solution.py:121
  715.3 41.4 %psum.7 = f32[2]{0:T(128)S(1)} all-reduce(f32[2]{0:T(128)S(1)} %pad_maximum_fusion), channel_id=1, replica_groups=mesh['row'=8,'col'=4] {'row','col'}, use_global_device_ids=true, to_apply=%region_2.3 | all-reduce | flops 2 | bytes 16 | tf_op jit(solution)/shard_map/psum | solution.py:124
  (149 shorter events, 218.5 us)
Async XLA Ops:
  0.6 216.8 %copy-start = (f32[4,4]{1,0:T(4,128)S(1)}, f32[4,4]{1,0:T(4,128)}, u32[]{:S(2)}) copy-start(f32[4,4]{1,0:T(4,128)} %param.11) | copy-start | bytes 196
  0.6 6.2 copy-start.21
  26.8 50.9 %all-to-all-start.2 = ((f32[8,1,256,256]{2,3,1,0:T(8,128)}), f32[8,1,256,256]{2,3,1,0:T(8,128)}, u32[]{:S(2)}, u32[]{:S(2)}) async-start(f32[8,1,256,256]{2,3,1,0:T(8,128)} %copy.210), calls=%async_computation.2 | async-start | bytes 4194304 | tf_op jit(solution)/shard_map/all_to_all | solution.py:83
  38.2 2.2 copy-start.15
  77.8 53.4 %all-to-all-start = ((f32[1,2048,256]{2,0,1:T(1,128)}), f32[1,2048,256]{2,0,1:T(1,128)}, u32[]{:S(2)}, u32[]{:S(2)}) async-start(f32[1,2048,256]{2,0,1:T(1,128)} %add_bitcast_fusion.1), calls=%async_computation | async-start | bytes 4194304 | tf_op jit(solution)/shard_map/all_to_all | solution.py:69
  131.1 31.6 %all-to-all-start.3 = ((f32[1,256,2048]{2,0,1:T(1,128)}), f32[1,256,2048]{2,0,1:T(1,128)}, u32[]{:S(2)}, u32[]{:S(2)}) async-start(f32[1,256,2048]{2,0,1:T(1,128)} %copy.212), calls=%async_computation.3 | async-start | bytes 4194304 | tf_op jit(solution)/shard_map/all_to_all | solution.py:81
  162.8 29.9 %all-to-all-start.1 = ((f32[1,256,2048]{2,0,1:T(1,128)}), f32[1,256,2048]{2,0,1:T(1,128)}, u32[]{:S(2)}, u32[]{:S(2)}) async-start(f32[1,256,2048]{2,0,1:T(1,128)} %copy.209), calls=%async_computation.1 | async-start | bytes 4194304 | tf_op jit(solution)/shard_map/all_to_all | solution.py:68
  192.7 2.6 copy-start.17
  192.7 2.7 copy-start.19
  196.4 1.6 copy-start.4
  200.9 1.3 copy-start.12
  311.4 29.6 %all-to-all-start.5 = ((f32[4,512,256]{2,1,0:T(8,128)}), f32[4,512,256]{2,1,0:T(8,128)}, u32[]{:S(2)}, u32[]{:S(2)}) async-start(f32[4,512,256]{2,1,0:T(8,128)} %bitcast.234), calls=%async_computation.5 | async-start | bytes 4194304 | tf_op jit(solution)/shard_map/all_to_all | solution.py:106
  341.0 2.2 copy-start.5
  345.5 1.3 copy-start.13
  349.0 2.2 copy-start.8
  349.0 2.8 copy-start.10
  364.3 2.3 copy-start.1
  375.8 52.2 %all-to-all-start.8 = ((f32[8,1,256,256]{2,3,1,0:T(8,128)}), f32[8,1,256,256]{2,3,1,0:T(8,128)}, u32[]{:S(2)}, u32[]{:S(2)}) async-start(f32[8,1,256,256]{2,3,1,0:T(8,128)} %copy.232), calls=%async_computation.8 | async-start | bytes 4194304 | tf_op jit(solution)/shard_map/all_to_all | solution.py:83
  382.4 4.5 copy-start.2
  382.4 4.5 copy-start.16
  427.9 53.4 %all-to-all-start.6 = ((f32[1,2048,256]{2,0,1:T(1,128)}), f32[1,2048,256]{2,0,1:T(1,128)}, u32[]{:S(2)}, u32[]{:S(2)}) async-start(f32[1,2048,256]{2,0,1:T(1,128)} %add_bitcast_fusion), calls=%async_computation.6 | async-start | bytes 4194304 | tf_op jit(solution)/shard_map/all_to_all | solution.py:69
  481.4 29.9 %all-to-all-start.9 = ((f32[1,256,2048]{2,0,1:T(1,128)}), f32[1,256,2048]{2,0,1:T(1,128)}, u32[]{:S(2)}, u32[]{:S(2)}) async-start(f32[1,256,2048]{2,0,1:T(1,128)} %copy.234), calls=%async_computation.9 | async-start | bytes 4194304 | tf_op jit(solution)/shard_map/all_to_all | solution.py:81
  511.2 29.2 %all-to-all-start.7 = ((f32[1,256,2048]{2,0,1:T(1,128)}), f32[1,256,2048]{2,0,1:T(1,128)}, u32[]{:S(2)}, u32[]{:S(2)}) async-start(f32[1,256,2048]{2,0,1:T(1,128)} %copy.231), calls=%async_computation.7 | async-start | bytes 4194304 | tf_op jit(solution)/shard_map/all_to_all | solution.py:68
  540.4 2.6 copy-start.18
  540.4 2.7 copy-start.20
  544.2 1.6 copy-start.6
  548.7 1.3 copy-start.14
  687.4 1.6 copy-start.7
  691.3 1.4 copy-start.11
  694.8 2.2 copy-start.3
  694.8 2.8 copy-start.9
